TPU v7x, 32 devices: a whole 2x2x4 slice. The times are simulated.
32 devices in a mesh: lb: 2 (over y), rb: 4 (over z), wa: 4 (over x, core).
Axes of the slice: x: 2, y: 2, z: 4, core: 2. Of those that a mesh axis runs over, the one named last changes fastest.
Arguments:
- state: bfloat16 [4, 4, 4, 1024, 1024], P('wa', None, None, 'lb', 'rb'), may hold values from -14 to 14
- left_env: bfloat16 [3, 4, 1024, 4, 1024], P(None, None, 'lb', 'wa'), may hold values from -1 to 2.5
- right_env: bfloat16 [3, 4, 1024, 4, 1024], P(None, None, 'rb', 'wa'), may hold values from -1 to 2.5
- site_one: float32 [3, 3, 2, 2], replicated, may hold values from -2 to 3
- site_two: float32 [3, 3, 2, 2], replicated, may hold values from -2 to 3
Outputs:
- next_vector: float32 [4, 4, 4, 1024, 1024], P('wa', None, None, 'lb', 'rb')
- coefficients: float32 [2], replicated
All inputs are finite; a program needn't handle non-finite values.
Results may differ from a plain program's by a relative error of at most 0.02.
Values may be sent and summed in bfloat16 or wider, within the bound.
A program may use at most 192 MiB of HBM per device.

v0:
```python
import functools
import jax
import jax.numpy as jnp
from jax import lax
from jax.experimental import pallas as pl
from jax.experimental.pallas import tpu as pltpu
from jax.sharding import PartitionSpec as P

EPSILON = 1e-06
CHUNKS = 4
GATHERS = 2


def pair_tensor(site_one, site_two):
    joined = jnp.einsum("wuac,uvbd->wvabcd", site_one, site_two, precision=lax.Precision.HIGHEST)
    mpo_width = site_one.shape[0]
    states = site_one.shape[2] * site_two.shape[2]
    return joined.reshape(mpo_width, mpo_width, states, states)


def mix_kernel(terms, pair_ref, *refs):
    out_ref = refs[terms]
    width, _, states, rows, _ = refs[0].shape
    step = 16

    @pl.loop(0, rows // step)
    def _(block):
        span = pl.ds(pl.multiple_of(block * step, step), step)
        planes = []
        for w in range(width):
            for s in range(states):
                value = refs[0][w, 0, s, span, :].astype(jnp.float32)
                for other in refs[1:terms]:
                    value = value + other[w, 0, s, span, :].astype(jnp.float32)
                planes.append(value)
        for v in range(width):
            for t in range(states):
                total = None
                for w in range(width):
                    for s in range(states):
                        entry = pair_ref[((w * width + v) * states + s) * states + t]
                        term = planes[w * states + s] * entry
                        total = term if total is None else total + term
                out_ref[v, 0, t, span, :] = total.astype(out_ref.dtype)


def mix(pair, parts):
    width, blocks, states, rows, lanes = parts[0].shape
    spec = pl.BlockSpec((width, 1, states, rows, lanes), lambda h: (0, h, 0, 0, 0))
    count = width * states
    size = parts[0].size
    return pl.pallas_call(
        functools.partial(mix_kernel, len(parts)),
        grid=(blocks,),
        out_shape=jax.ShapeDtypeStruct(parts[0].shape, jnp.bfloat16),
        in_specs=[pl.BlockSpec(memory_space=pltpu.SMEM)] + [spec] * len(parts),
        out_specs=spec,
        cost_estimate=pl.CostEstimate(
            flops=2 * size * count * 16, bytes_accessed=2 * size * (len(parts) + 1), transcendentals=0
        ),
    )(pair.reshape(-1), *parts)


def body(state, left_env, right_env, site_one, site_two):
    pair = pair_tensor(site_one, site_two)
    lefts, rights, owners = (lax.axis_size(name) for name in ("lb", "rb", "wa"))
    mine = lax.axis_index("lb")
    here = lax.axis_index("wa")
    _, blocks, _, _, _ = state.shape
    entries = float(state.size * lefts * rights * owners)

    group = blocks // GATHERS
    gathered = []
    for h in range(0, blocks, group):
        gathered.append(lax.all_gather(state[:, h : h + group], "wa", axis=0, tiled=True))
    turned = jnp.transpose(left_env[:, :, :, 0, :], (0, 1, 3, 2))
    owned = turned.shape[2] // lefts
    chunk = owned // CHUNKS

    def left_part(owner, position):
        rows = lax.dynamic_slice_in_dim(turned, owner * owned + position * chunk, chunk, 2)
        return [
            jnp.einsum(
                "wgpm,ghsmn->whspn", rows, part, preferred_element_type=jnp.float32
            ).astype(jnp.bfloat16)
            for part in gathered
        ]

    envs = {0: right_env[:, :, :, 0, :]}
    bit = owners // 2
    while bit:
        swap = [(a, a ^ bit) for a in range(owners)]
        for r in list(envs):
            envs[r ^ bit] = lax.ppermute(envs[r], "wa", swap)
        bit //= 2
    order = sorted(envs)
    near, far = order[: owners // 2], order[owners // 2 :]
    width, wide = envs[0].shape[0], envs[0].shape[3]

    def joined(pack):
        env = jnp.concatenate([envs[r] for r in pack], axis=3)
        return env.reshape(width, blocks, -1, len(pack), wide)

    packs = [(pack, joined(pack)) for pack in (near, far, order)]

    images = {r: [] for r in order}
    for position in range(CHUNKS):
        arrived = []
        for shift in range(1, lefts):
            sent = left_part(lax.rem(mine + shift, lefts), position)
            ring = [(a, (a + shift) % lefts) for a in range(lefts)]
            arrived.append([lax.ppermute(piece, "lb", ring) for piece in sent])
        parts = [jnp.concatenate(p, axis=1) for p in [left_part(mine, position)] + arrived]
        mixed = mix(pair, parts)
        for pack, env in packs[:2] if position == 0 else packs[2:]:
            part = jnp.einsum("vhtpn,vhndq->dtpq", mixed, env, preferred_element_type=jnp.float32).astype(jnp.bfloat16)
            part = lax.psum_scatter(part, "rb", scatter_dimension=3, tiled=True)
            for r, piece in zip(pack, part):
                images[r].append(piece)
    applied = [jnp.concatenate(images[r], axis=1).astype(jnp.float32) for r in order]
    vectors = [
        lax.dynamic_index_in_dim(state[0], here ^ r, 0, keepdims=False).astype(jnp.float32)
        for r in order
    ]
    state_values = state.astype(jnp.float32)
    terms = jnp.stack(
        [
            jnp.sum(state_values * state_values),
            sum(jnp.sum(s * a) for s, a in zip(vectors, applied)),
            sum(jnp.sum(a * a) for a in applied),
        ]
    )
    for name in ("wa", "lb", "rb"):
        size, bit = lax.axis_size(name), 1
        while bit < size:
            terms = terms + lax.ppermute(terms, name, [(a, a ^ bit) for a in range(size)])
            bit *= 2
    squares, crossed, image_squares = terms
    norm_sq = squares / entries + EPSILON
    projection = crossed / entries
    alpha_coef = projection / norm_sq
    beta_coef = jnp.sqrt((image_squares / entries - alpha_coef * projection) / norm_sq + EPSILON)
    scale = 1.0 / (jnp.sqrt(norm_sq) * beta_coef)
    result = jnp.zeros(state.shape, jnp.float32)
    for r, s, a in zip(order, vectors, applied):
        value = (a - alpha_coef * s) * scale
        result = lax.dynamic_update_slice(result, value[None, None], (0, here ^ r, 0, 0, 0))
    return (result, jnp.stack([alpha_coef, beta_coef]))


MESH = pl.DeviceIdType.MESH
STEP = 32
DEPTH = 8
HOP = 2


def line_kernel(
    sizes,
    pair_ref,
    own_ref,
    near_ref,
    far_ref,
    env_ref,
    right_ref,
    out_ref,
    psi,
    images,
    mixed,
    rows_buf,
    parts,
    arrived,
    sums,
    from_low,
    from_high,
    done,
    load_sem,
    psi_send,
    psi_recv,
    right_load,
    right_send,
    right_recv,
    rows_sem,
    part_send,
    part_recv,
    sum_send,
    low_recv,
    high_recv,
    low_free,
    high_free,
    done_sem,
):
    width, blocks, states, depth, line = sizes
    chunks = env_ref.shape[0]
    units = 4 * chunks
    early = chunks // 4
    pairs = blocks * states
    mine = lax.axis_index("lb")
    place = lax.axis_index("rb")
    here = lax.axis_index("wa")
    beside = here + 1 - 2 * lax.rem(here, 2)
    across = lax.rem(here + 2, 4)
    corner = 3 - here
    partner = (mine, place, beside)
    opposite = (mine, place, across)
    other = (1 - mine, place, here)
    higher = (mine, lax.rem(place + 1, line), here)
    lower = (mine, lax.rem(place + line - 1, line), here)

    local = []
    for n, (source, owner) in enumerate(((own_ref, here), (near_ref, beside), (far_ref, across))):
        span = pl.ds(pl.multiple_of(owner * depth, depth), depth)
        local.append(pltpu.make_async_copy(source, psi.at[:, span, :], load_sem.at[n]))
    lanes = right_ref.shape[1] // line
    half = lanes // 2
    for part in range(2):
        for d in range(line):
            local.append(
                pltpu.make_async_copy(
                    right_ref.at[:, pl.ds(d * lanes + part * half, half)],
                    images.at[part, :, pl.ds(d * half, half)],
                    right_load.at[part, d],
                )
            )
    for copy in local:
        copy.start()

    barrier = pltpu.get_barrier_semaphore()
    for device in (partner, opposite, other, higher, lower):
        pl.semaphore_signal(barrier, inc=1, device_id=device, device_id_type=MESH)
    pl.semaphore_wait(barrier, 5)

    def remote(source, target, send, recv, device):
        return pltpu.make_async_remote_copy(
            src_ref=source, dst_ref=target, send_sem=send, recv_sem=recv, device_id=device, device_id_type=MESH
        )

    span = pl.ds(pl.multiple_of(across * depth, depth), depth)
    relay = remote(far_ref, psi.at[:, span, :], psi_send.at[0], psi_recv.at[0], partner)
    relay.start()

    def rows_copy(c):
        slot = lax.rem(c, 2)
        return pltpu.make_async_copy(env_ref.at[c], rows_buf.at[slot], rows_sem.at[slot])

    rows_copy(0).start()
    for copy in local:
        copy.wait()

    def image_copy(n, source, target, device):
        return remote(images.at[source], images.at[target], right_send.at[n], right_recv.at[n], device)

    beside_copies = [image_copy(0, 0, 2, partner), image_copy(1, 1, 3, partner)]
    across_copies = [image_copy(2, 0, 4, opposite), image_copy(3, 1, 6, opposite)]
    corner_copies = [image_copy(4, 4, 5, partner), image_copy(5, 6, 7, partner)]
    for copy in across_copies + beside_copies:
        copy.start()
    relay.wait()

    def part_copy(c):
        slot = lax.rem(c, 2)
        target = lax.rem(c, 4)
        return remote(
            parts.at[slot, 1 - mine], arrived.at[target], part_send.at[slot], part_recv.at[target], other
        )

    def left(c):
        slot = lax.rem(c, 2)

        @pl.when(c >= 2)
        def _():
            part_copy(c - 2).wait_send()

        rows_copy(c).wait()

        @pl.when(c + 1 < chunks)
        def _():
            rows_copy(c + 1).start()

        def one(p, carry):
            value = jnp.dot(rows_buf[slot], psi[p], preferred_element_type=jnp.float32)
            value = value.astype(jnp.bfloat16)
            rows = value.shape[0] // 2
            parts[slot, 0, p] = value[:rows]
            parts[slot, 1, p] = value[rows:]
            return carry

        lax.fori_loop(0, pairs, one, 0)
        part_copy(c).start()

    def front(c):
        @pl.when(c + 1 < chunks)
        def _():
            left(c + 1)

        part_copy(c).wait_recv()
        slot = lax.rem(c, 2)
        source = lax.rem(c, 4)
        target = lax.rem(c, DEPTH)
        tile = 16
        wide = psi.shape[2]

        def one(h, carry):
            for step in range(STEP // tile):
                planes = []
                for w in range(width):
                    for s in range(states):
                        span = pl.ds(w * STEP + step * tile, tile)
                        value = parts[slot, mine, h * states + s, span, :].astype(jnp.float32)
                        value = value + arrived[source, h * states + s, span, :].astype(jnp.float32)
                        planes.append(value)
                for v in range(width):
                    for t in range(states):
                        total = None
                        for w in range(width):
                            for s in range(states):
                                entry = pair_ref[((w * width + v) * states + s) * states + t]
                                term = planes[w * states + s] * entry
                                total = term if total is None else total + term
                        column = pl.multiple_of((v * blocks + h) * wide, wide)
                        mixed[target, pl.ds(t * STEP + step * tile, tile), pl.ds(column, wide)] = total.astype(
                            jnp.bfloat16
                        )
            return carry

        lax.fori_loop(0, blocks, one, 0)

    def up_copy(u, d):
        slot = lax.rem(u, DEPTH)
        return remote(sums.at[slot, d], from_low.at[slot, d], sum_send.at[slot, d], low_recv.at[slot, d], higher)

    def down_copy(u, d):
        slot = lax.rem(u, DEPTH)
        return remote(sums.at[slot, d], from_high.at[slot, d], sum_send.at[slot, d], high_recv.at[slot, d], lower)

    def drained(u):
        for d in range(line):

            @pl.when(d > place)
            def _():
                up_copy(u, d).wait_send()

            @pl.when(d < place)
            def _():
                down_copy(u, d).wait_send()

    def added(slot, d, source):
        total = sums[slot, d].astype(jnp.float32) + source[slot, d].astype(jnp.float32)
        sums[slot, d] = total.astype(jnp.bfloat16)

    def where_to(u):
        near = jnp.where(u < 2 * early, 1, 0)
        first = jnp.where(u < 3 * early, 1, 0)
        second = jnp.where(u < 6 * early, 1, 0)
        third = jnp.where(u < 8 * early, 1, 0)
        a, b, e, g = u, u - 2 * early, u - 3 * early, u - 6 * early
        f = u - 8 * early
        chunk = jnp.where(
            near == 1,
            a // 2,
            jnp.where(
                first == 1,
                b,
                jnp.where(second == 1, early + e // 3, jnp.where(third == 1, g, 2 * early + f // 4)),
            ),
        )
        kind = jnp.where(
            near == 1,
            lax.rem(a, 2),
            jnp.where(
                first == 1, 2, jnp.where(second == 1, lax.rem(e + 3 * units, 3), jnp.where(third == 1, 3, lax.rem(f + 8 * units, 4)))
            ),
        )
        return chunk, kind

    def done_copies(u):
        slot = lax.rem(u, 2)
        chunk, kind = where_to(u)
        far = kind // 2
        near_block = here + kind * (beside - here)
        copies = []
        for j in range(2):
            far_block = corner if j else across
            block = (1 - far) * near_block + far * far_block
            column = (1 - far) * j + far * (kind - 2)
            copies.append(
                pltpu.make_async_copy(
                    done.at[slot, j],
                    out_ref.at[
                        block,
                        :,
                        pl.ds(pl.multiple_of(chunk * STEP, STEP), STEP),
                        pl.ds(pl.multiple_of(column * half, half), half),
                    ],
                    done_sem.at[slot, j],
                )
            )
        return copies

    def handle(i):
        up = i - HOP * place
        slot_up = lax.rem(up + DEPTH * HOP * line, DEPTH)

        @pl.when(jnp.logical_and(place < line - 1, jnp.logical_and(up >= 0, up < units)))
        def _():
            @pl.when(up >= DEPTH)
            def _():
                pl.semaphore_wait(high_free, 1)

            for d in range(line - 1, 0, -1):

                @pl.when(d > place)
                def _():
                    @pl.when(place > 0)
                    def _():
                        up_copy(up, d).wait_recv()
                        added(slot_up, d, from_low)

                    up_copy(up, d).start()

        down = i - HOP * (line - 1 - place)
        slot_down = lax.rem(down + DEPTH * HOP * line, DEPTH)

        @pl.when(jnp.logical_and(place > 0, jnp.logical_and(down >= 0, down < units)))
        def _():
            @pl.when(down >= DEPTH)
            def _():
                pl.semaphore_wait(low_free, 1)

            for d in range(line - 1):

                @pl.when(d < place)
                def _():
                    @pl.when(place < line - 1)
                    def _():
                        down_copy(down, d).wait_recv()
                        added(slot_down, d, from_high)

                    down_copy(down, d).start()

        last = i - HOP * (line - 1)

        @pl.when(last >= 0)
        def _():
            slot = lax.rem(last, DEPTH)
            spot = lax.rem(last, 2)

            @pl.when(last >= 2)
            def _():
                for copy in done_copies(last - 2):
                    copy.wait()

            shape = done.shape[1:]
            value = sums[slot, place].astype(jnp.float32)
            done[spot] = value.reshape(shape)

            @pl.when(place > 0)
            def _():
                up_copy(last, place).wait_recv()
                more = from_low[slot, place].astype(jnp.float32)
                done[spot] = done[spot] + more.reshape(shape)

                @pl.when(last < units - DEPTH)
                def _():
                    pl.semaphore_signal(high_free, inc=1, device_id=lower, device_id_type=MESH)

            @pl.when(place < line - 1)
            def _():
                down_copy(last, place).wait_recv()
                more = from_high[slot, place].astype(jnp.float32)
                done[spot] = done[spot] + more.reshape(shape)

                @pl.when(last < units - DEPTH)
                def _():
                    pl.semaphore_signal(low_free, inc=1, device_id=higher, device_id_type=MESH)

            for copy in done_copies(last):
                copy.start()

    def unit(u, c, kind):
        slot = lax.rem(u, DEPTH)

        @pl.when(u >= DEPTH)
        def _():
            drained(u - DEPTH)

        source = lax.rem(c, DEPTH)

        def one(j, carry):
            value = jnp.dot(mixed[source], images[2 * kind + j], preferred_element_type=jnp.float32)
            value = value.astype(jnp.bfloat16)
            for d in range(line):
                sums[slot, d, j] = value[:, d * half : (d + 1) * half]
            return carry

        lax.fori_loop(0, 2, one, 0)
        handle(u)

    def walk(start, base, kinds, fresh):
        def one(n, carry):
            c = start + n
            if fresh:
                front(c)

            def inner(k, carry):
                unit(base + n * len(kinds) + k, c, kinds[0] + k)
                return carry

            lax.fori_loop(0, len(kinds), inner, 0)
            return carry

        return one

    left(0)
    for copy in beside_copies:
        copy.wait()
    lax.fori_loop(0, early, walk(0, 0, (0, 1), True), 0)
    across_copies[0].wait()
    corner_copies[0].start()
    corner_copies[0].wait()
    lax.fori_loop(0, early, walk(0, 2 * early, (2,), False), 0)
    lax.fori_loop(0, early, walk(early, 3 * early, (0, 1, 2), True), 0)
    across_copies[1].wait()
    corner_copies[1].start()
    corner_copies[1].wait()
    lax.fori_loop(0, 2 * early, walk(0, 6 * early, (3,), False), 0)
    lax.fori_loop(0, 2 * early, walk(2 * early, 8 * early, (0, 1, 2, 3), True), 0)

    def finish(i, carry):
        handle(i)
        return carry

    lax.fori_loop(units, units + HOP * (line - 1), finish, 0)
    for u in range(units - DEPTH, units):
        drained(u)
    for u in range(units - 2, units):
        for copy in done_copies(u):
            copy.wait()
    for c in range(chunks - 2, chunks):
        part_copy(c).wait_send()


def line_call(pair, own, near, far, env, right, line):
    pairs, depth, wide = own.shape
    chunks, rows, inner = env.shape
    width = rows // (2 * STEP)
    blocks = inner // depth
    states = pairs // blocks
    lanes = right.shape[1] // line
    half = lanes // 2
    tall = states * STEP
    low = jnp.bfloat16
    hbm = pl.BlockSpec(memory_space=pltpu.MemorySpace.HBM)
    dma = pltpu.SemaphoreType.DMA
    plain = pltpu.SemaphoreType.REGULAR
    return pl.pallas_call(
        functools.partial(line_kernel, (width, blocks, states, depth, line)),
        out_shape=jax.ShapeDtypeStruct((blocks, states, chunks * STEP, lanes), jnp.float32),
        in_specs=[pl.BlockSpec(memory_space=pltpu.SMEM)] + [hbm] * 5,
        out_specs=hbm,
        scratch_shapes=[
            pltpu.VMEM((pairs, inner, wide), low),
            pltpu.VMEM((8, right.shape[0], line * half), low),
            pltpu.VMEM((DEPTH, tall, right.shape[0]), low),
            pltpu.VMEM((2, rows, inner), low),
            pltpu.VMEM((2, 2, pairs, rows // 2, wide), low),
            pltpu.VMEM((4, pairs, rows // 2, wide), low),
            pltpu.VMEM((DEPTH, line, 2, tall, half), low),
            pltpu.VMEM((DEPTH, line, 2, tall, half), low),
            pltpu.VMEM((DEPTH, line, 2, tall, half), low),
            pltpu.VMEM((2, 2, states, STEP, half), jnp.float32),
            dma((3,)),
            dma((1,)),
            dma((1,)),
            dma((2, line)),
            dma((6,)),
            dma((6,)),
            dma((2,)),
            dma((2,)),
            dma((4,)),
            dma((DEPTH, line)),
            dma((DEPTH, line)),
            dma((DEPTH, line)),
            plain,
            plain,
            dma((2, 2)),
        ],
        compiler_params=pltpu.CompilerParams(
            collective_id=0, has_side_effects=True, vmem_limit_bytes=67043328
        ),
        cost_estimate=pl.CostEstimate(
            flops=2 * chunks * (rows * inner * pairs * wide + tall * right.shape[0] * 4 * line * lanes),
            bytes_accessed=2 * (env.size + 3 * own.size + right.size) + 4 * chunks * tall * blocks * lanes,
            transcendentals=0,
        ),
    )(pair.reshape(-1), own, near, far, env, right)


def lined_body(state, left_env, right_env, site_one, site_two):
    pair = pair_tensor(site_one, site_two)
    lefts, rights, owners = (lax.axis_size(name) for name in ("lb", "rb", "wa"))
    _, blocks, states, depth, lanes = state.shape
    entries = float(state.size * lefts * rights * owners)
    width, _, _, _, rows = left_env.shape
    own = state.reshape(blocks * states, depth, lanes)
    far = lax.ppermute(own, "wa", [(a, (a + 2) % 4) for a in range(owners)])
    near = lax.ppermute(own, "wa", [(a, a ^ 1) for a in range(owners)])
    chunks = rows // (lefts * STEP)
    env = left_env.reshape(width, blocks, depth, lefts, chunks, STEP)
    env = jnp.transpose(env, (4, 3, 0, 5, 1, 2)).reshape(chunks, lefts * width * STEP, blocks * depth)
    right = right_env.reshape(-1, right_env.shape[-1])
    applied = line_call(pair, own, near, far, env, right, rights)
    state_values = state[0].astype(jnp.float32)
    terms = jnp.stack(
        [
            jnp.sum(state_values * state_values),
            jnp.sum(state_values * applied),
            jnp.sum(applied * applied),
        ]
    )
    for name in ("wa", "lb", "rb"):
        size, bit = lax.axis_size(name), 1
        while bit < size:
            terms = terms + lax.ppermute(terms, name, [(a, a ^ bit) for a in range(size)])
            bit *= 2
    squares, crossed, image_squares = terms
    norm_sq = squares / entries + EPSILON
    projection = crossed / entries
    alpha_coef = projection / norm_sq
    beta_coef = jnp.sqrt((image_squares / entries - alpha_coef * projection) / norm_sq + EPSILON)
    scale = 1.0 / (jnp.sqrt(norm_sq) * beta_coef)
    result = (applied - alpha_coef * state_values) * scale
    return (result[None], jnp.stack([alpha_coef, beta_coef]))


def fits(mesh):
    return (mesh.shape["lb"], mesh.shape["rb"], mesh.shape["wa"]) == (2, 4, 4)


def solution(mesh):
    placed = (
        P("wa", None, None, "lb", "rb"),
        P(None, None, "lb", "wa", None),
        P(None, None, "rb", "wa", None),
        P(),
        P(),
    )
    if fits(mesh):
        return jax.shard_map(
            lined_body,
            mesh=mesh,
            in_specs=placed,
            out_specs=(P("wa", None, None, "lb", "rb"), P()),
            check_vma=False,
        )
    return jax.shard_map(
        body,
        mesh=mesh,
        in_specs=placed,
        out_specs=(P("wa", None, None, "lb", "rb"), P()),
        check_vma=False,
    )
```

profile of v0, /device:TPU:0, one launch (start us, length us, event | category | flops | bytes accessed | tf_op | source)
XLA Modules:
  0.0 494.9 jit_solution(1865537448530284647)
XLA Ops:
  0.6 0.6 collective-permute-start
  1.2 2.6 collective-permute-start.1
  3.7 16.9 %copy.13 = bf16[3,4,512,1,1024]{2,4,1,0,3:T(8,128)(2,1)} copy(bf16[3,4,512,1,1024]{4,2,3,1,0:T(8,128)(2,1)} %param.6) | data formatting | bytes 25165824 | tf_op args[1]
  20.7 15.6 %copy.14 = bf16[16,2,3,32,4,512]{5,4,3,2,1,0:T(4,128)(2,1)} copy(bf16[16,2,3,32,4,512]{5,3,0,1,4,2:T(8,128)(2,1)} %bitcast.24) | data formatting | bytes 25165824 | tf_op jit(solution)/shard_map/transpose | solution.py:609
  36.3 20.9 %reshape.28.env_ref = bf16[16,192,2048]{2,1,0:T(8,128)(2,1)} reshape(bf16[16,2,3,32,4,512]{5,4,3,2,1,0:T(4,128)(2,1)} %copy.14) | data formatting | bytes 25165824 | tf_op jit(solution)/shard_map/reshape | solution.py:609
  57.2 0.4 convolution_bitcast_fusion
  57.9 0.7 reshape_reshape.3.pair_ref
  58.6 36.6 %collective-permute-done.1.far_ref = bf16[16,512,256]{2,1,0:T(8,128)(2,1)} collective-permute-done((bf16[16,512,256]{2,1,0:T(8,128)(2,1)}, bf16[16,512,256]{2,1,0:T(8,128)(2,1)}, u32[]{:S(2)}, u32[]{:S(2)}) %collective-permute-start.1) | collective-permute-done | bytes 4194336 | tf_op jit(solution)/shard_map/ppermute | solution.py:605
  95.2 358.3 %shard_map.68 = f32[4,4,512,256]{3,2,1,0:T(8,128)} custom-call(f32[144]{0:T(256)} %reshape_reshape.3.pair_ref, bf16[16,512,256]{2,1,0:T(8,128)(2,1)} %bitcast.27, bf16[16,512,256]{2,1,0:T(8,128)(2,1)} %collective-permute-done.near_ref, bf16[16,512,256]{2,1,0:T(8,128)(2,1)} %collective-permute-done.1.far_ref, bf16[16,192,2048]{2,1,0:T(8,128)(2,1)} %reshape.28.env_ref, ...), custom_call_target="tpu_custom_call" | custom-call | flops 103079215104 | bytes 39845888 | tf_op jit(solution)/shard_map/pallas_call | solution.py:555
  453.5 6.4 %fusion.1 = (f32[]{:T(128)}, f32[]{:T(128)}, f32[]{:T(128)}) fusion(f32[4,4,512,256]{3,2,1,0:T(8,128)} %shard_map.68, bf16[1,4,4,512,256]{4,3,2,1,0:T(8,128)(2,1)} %param.5), kind=kLoop, calls=%fused_computation.4 | loop fusion | flops 14680061 | bytes 12582924 | tf_op jit(solution)/shard_map/reduce_sum | solution.py:616
  459.9 2.0 pad_maximum_fusion
  461.9 1.1 collective-permute-done.2
  463.1 2.0 fusion.8
  465.1 1.6 collective-permute-start.3
  466.7 2.0 collective-permute-done.3
  468.7 2.0 fusion.9
  470.7 1.3 collective-permute-start.4
  472.0 2.2 collective-permute-done.4
  474.2 3.6 collective-permute-done.5
  477.8 0.8 collective-permute-start.6
  478.6 3.6 collective-permute-done.6
  482.3 0.7 fusion.7
  485.1 9.2 %fusion.4 = f32[1,4,4,512,256]{4,3,2,1,0:T(8,128)} fusion(f32[4,4,512,256]{3,2,1,0:T(8,128)} %shard_map.68, bf16[1,4,4,512,256]{4,3,2,1,0:T(8,128)(2,1)} %param.5, f32[]{:T(128)S(6)} %div.29, f32[]{:T(128)} %div.25), kind=kLoop, calls=%fused_computation.7 | loop fusion | flops 8388608 | bytes 20971528 | tf_op jit(solution)/shard_map/broadcast_in_dim | solution.py:632
  494.3 0.6 pad_maximum_fusion.1
  (11 shorter events, 0.3 us)
Async XLA Ops:
  0.6 58.0 %collective-permute-start = (bf16[16,512,256]{2,1,0:T(8,128)(2,1)}, bf16[16,512,256]{2,1,0:T(8,128)(2,1)}, u32[]{:S(2)}, u32[]{:S(2)}) collective-permute-start(bf16[16,512,256]{2,1,0:T(8,128)(2,1)} %bitcast.25), channel_id=1, source_target_pairs={{0,1},{1,0},{2,3},{3,2},{4,5},{5,4},{6,7},{7,6},{8,9},{9,8},{10,11... | collective-permute-start | bytes 12582920 | tf_op jit(solution)/shard_map/ppermute | solution.py:606
  1.2 94.0 %collective-permute-start.1 = (bf16[16,512,256]{2,1,0:T(8,128)(2,1)}, bf16[16,512,256]{2,1,0:T(8,128)(2,1)}, u32[]{:S(2)}, u32[]{:S(2)}) collective-permute-start(bf16[16,512,256]{2,1,0:T(8,128)(2,1)} %bitcast.26), channel_id=1, source_target_pairs={{0,2},{1,3},{2,0},{3,1},{4,6},{5,7},{6,4},{7,5},{8,10},{9,11},{10,... | collective-permute-start | bytes 12582920 | tf_op jit(solution)/shard_map/ppermute | solution.py:605
  36.3 20.9 %copy-start = (f32[3,3,2,2]{1,3,2,0:T(2,128)S(1)}, f32[3,3,2,2]{1,3,2,0:T(2,128)}, u32[]{:S(2)}) copy-start(f32[3,3,2,2]{1,3,2,0:T(2,128)} %param.8) | copy-start | bytes 436
  36.3 20.9 %copy-start.1 = (f32[3,3,2,2]{1,3,2,0:T(2,128)S(1)}, f32[3,3,2,2]{1,3,2,0:T(2,128)}, u32[]{:S(2)}) copy-start(f32[3,3,2,2]{1,3,2,0:T(2,128)} %param.9) | copy-start | bytes 436
  461.9 1.2 collective-permute-start.2
  465.1 3.6 collective-permute-start.3
  470.7 3.6 collective-permute-start.4
  474.2 3.6 collective-permute-start.5
  477.8 4.5 collective-permute-start.6
where the time goes:
time: 496 us; the launch traced here: 495 us
  Pallas kernels  358 us (72%)
  local copies, waits for them, and re-layouts  55.1 us (11%)
  waiting for transfers between devices  49.2 us (10%)
  other arithmetic  22.3 us (4%)
  starting transfers between devices  6.86 us (1%)
    pallas_call x1, Pallas kernels, line_call(): pl.pallas_call(functools.partial(line_kernel, (width, blocks, states, dep...  358 us
    ppermute x1, waiting for transfers between devices, lined_body(): far = lax.ppermute(own, 'wa', [(a, (a + 2) % 4) for a in range(owners)])  36.6 us
    reshape x1, local copies, waits for them, and re-layouts, lined_body(): jnp.transpose(env, (4, 3, 0, 5, 1, 2))  20.9 us
    unnamed x5, local copies, waits for them, and re-layouts  16.9 us
    transpose x1, local copies, waits for them, and re-layouts, lined_body(): jnp.transpose(env, (4, 3, 0, 5, 1, 2))  15.6 us
    ppermute x5, waiting for transfers between devices, lined_body(): lax.ppermute(terms, name, [(a, a ^ bit) for a in range(size)])  12.6 us
  transfers between devices with their start and end apart: 7, of which 6 were waited for; matrix products, arithmetic and copies ran while one was open for 11% of the time, Pallas kernels for 0%

commit v1 on v0

--- a/solution.py
+++ b/solution.py
@@ -152,20 +152,23 @@
 STEP = 32
 DEPTH = 8
 HOP = 2
+AHEAD = 3
+LANES = 128
 
 
 def line_kernel(
     sizes,
     pair_ref,
     own_ref,
-    near_ref,
-    far_ref,
-    env_ref,
+    left_ref,
     right_ref,
     out_ref,
+    env_ref,
+    total_ref,
     psi,
     images,
     mixed,
+    raw,
     rows_buf,
     parts,
     arrived,
@@ -173,27 +176,37 @@
     from_low,
     from_high,
     done,
+    terms,
+    heard,
     load_sem,
     psi_send,
     psi_recv,
+    relay_send,
+    relay_recv,
     right_load,
     right_send,
     right_recv,
+    raw_sem,
+    turn_sem,
     rows_sem,
     part_send,
     part_recv,
+    part_free,
     sum_send,
     low_recv,
     high_recv,
     low_free,
     high_free,
     done_sem,
+    term_send,
+    term_recv,
 ):
-    width, blocks, states, depth, line = sizes
+    width, blocks, states, depth, line, entries = sizes
     chunks = env_ref.shape[0]
     units = 4 * chunks
-    early = chunks // 4
-    pairs = blocks * states
+    early, middle = early_chunks(chunks)
+    kept = early + middle
+    inner = blocks * depth
     mine = lax.axis_index("lb")
     place = lax.axis_index("rb")
     here = lax.axis_index("wa")
@@ -205,13 +218,54 @@
     other = (1 - mine, place, here)
     higher = (mine, lax.rem(place + 1, line), here)
     lower = (mine, lax.rem(place + line - 1, line), here)
-
-    local = []
-    for n, (source, owner) in enumerate(((own_ref, here), (near_ref, beside), (far_ref, across))):
-        span = pl.ds(pl.multiple_of(owner * depth, depth), depth)
-        local.append(pltpu.make_async_copy(source, psi.at[:, span, :], load_sem.at[n]))
+    paired = (mine, place + 1 - 2 * lax.rem(place, 2), here)
+    distant = (mine, lax.rem(place + 2, line), here)
+
+    def remote(source, target, send, recv, device):
+        return pltpu.make_async_remote_copy(
+            src_ref=source, dst_ref=target, send_sem=send, recv_sem=recv, device_id=device, device_id_type=MESH
+        )
+
+    my_span = pl.ds(pl.multiple_of(here * depth, depth), depth)
+    across_span = pl.ds(pl.multiple_of(across * depth, depth), depth)
+    own_copy = pltpu.make_async_copy(own_ref, psi.at[:, my_span, :], load_sem.at[0])
+    own_copy.start()
+
+    def raw_copy(n):
+        slot = lax.rem(n, 2)
+        q = n // (2 * width)
+        side = lax.rem(n // width, 2)
+        w = lax.rem(n, width)
+        first = side * (chunks * STEP) + q * LANES
+        return pltpu.make_async_copy(
+            left_ref.at[pl.ds(pl.multiple_of(w * inner, inner), inner), pl.ds(pl.multiple_of(first, LANES), LANES)],
+            raw.at[slot],
+            raw_sem.at[slot],
+        )
+
+    raw_copy(0).start()
+
+    barrier = pltpu.get_barrier_semaphore()
+    devices = (partner, opposite, other, higher, lower, distant)
+    for device in devices:
+        pl.semaphore_signal(barrier, inc=1, device_id=device, device_id_type=MESH)
+    pl.semaphore_wait(barrier, len(devices))
+
+    def group(h):
+        return pl.ds(h * states, states)
+
+    psi_copies = [
+        remote(own_ref.at[group(h)], psi.at[group(h), my_span, :], psi_send.at[h], psi_recv.at[h], opposite)
+        for h in range(blocks)
+    ]
+    for copy in psi_copies:
+        copy.start()
+    share = remote(own_ref, psi.at[:, my_span, :], psi_send.at[blocks], psi_recv.at[blocks], partner)
+    share.start()
+
     lanes = right_ref.shape[1] // line
     half = lanes // 2
+    local = []
     for part in range(2):
         for d in range(line):
             local.append(
@@ -224,25 +278,69 @@
     for copy in local:
         copy.start()
 
-    barrier = pltpu.get_barrier_semaphore()
-    for device in (partner, opposite, other, higher, lower):
-        pl.semaphore_signal(barrier, inc=1, device_id=device, device_id_type=MESH)
-    pl.semaphore_wait(barrier, 5)
-
-    def remote(source, target, send, recv, device):
-        return pltpu.make_async_remote_copy(
-            src_ref=source, dst_ref=target, send_sem=send, recv_sem=recv, device_id=device, device_id_type=MESH
-        )
-
-    span = pl.ds(pl.multiple_of(across * depth, depth), depth)
-    relay = remote(far_ref, psi.at[:, span, :], psi_send.at[0], psi_recv.at[0], partner)
-    relay.start()
-
-    def rows_copy(c):
-        slot = lax.rem(c, 2)
+    turns = 2 * width * chunks * STEP // LANES
+    cuts = LANES // STEP
+
+    def turned_copies(n):
+        slot = lax.rem(n, 2)
+        q = n // (2 * width)
+        side = lax.rem(n // width, 2)
+        w = lax.rem(n, width)
+        first = (side * width + w) * STEP
+        return [
+            pltpu.make_async_copy(
+                mixed.at[slot, pl.ds(k * STEP, STEP), pl.ds(0, inner)],
+                env_ref.at[q * cuts + k, pl.ds(pl.multiple_of(first, STEP), STEP), :],
+                turn_sem.at[slot, k],
+            )
+            for k in range(cuts)
+        ]
+
+    def turn(n, carry):
+        slot = lax.rem(n, 2)
+
+        @pl.when(n + 1 < turns)
+        def _():
+            raw_copy(n + 1).start()
+
+        raw_copy(n).wait()
+
+        @pl.when(n >= 2)
+        def _():
+            for copy in turned_copies(n - 2):
+                copy.wait()
+
+        for g in range(blocks):
+            span = pl.ds(g * depth, depth)
+            mixed[slot, pl.ds(0, LANES), span] = raw[slot, span, :].T
+        for copy in turned_copies(n):
+            copy.start()
+        return carry
+
+    lax.fori_loop(0, turns, turn, 0)
+    for n in range(turns - 2, turns):
+        for copy in turned_copies(n):
+            copy.wait()
+
+    def rows_copy(n, c):
+        slot = lax.rem(n, 2)
         return pltpu.make_async_copy(env_ref.at[c], rows_buf.at[slot], rows_sem.at[slot])
 
-    rows_copy(0).start()
+    rows_copy(0, 0).start()
+    own_copy.wait()
+    terms[...] = jnp.zeros_like(terms)
+
+    def folded(value):
+        return jnp.sum(value.reshape(-1, 8, LANES), axis=0)
+
+    def square(p, carry):
+        value = psi[p, my_span, :].astype(jnp.float32)
+        value = value * value
+        for n in range(value.shape[1] // LANES):
+            terms[0] += folded(value[:, n * LANES : (n + 1) * LANES])
+        return carry
+
+    lax.fori_loop(0, blocks * states, square, 0)
     for copy in local:
         copy.wait()
 
@@ -252,54 +350,85 @@
     beside_copies = [image_copy(0, 0, 2, partner), image_copy(1, 1, 3, partner)]
     across_copies = [image_copy(2, 0, 4, opposite), image_copy(3, 1, 6, opposite)]
     corner_copies = [image_copy(4, 4, 5, partner), image_copy(5, 6, 7, partner)]
-    for copy in across_copies + beside_copies:
-        copy.start()
-    relay.wait()
-
-    def part_copy(c):
-        slot = lax.rem(c, 2)
-        target = lax.rem(c, 4)
+
+    def part_copy(c, h):
+        slot = lax.rem(c, AHEAD)
+        target = lax.rem(c, AHEAD + 1)
         return remote(
-            parts.at[slot, 1 - mine], arrived.at[target], part_send.at[slot], part_recv.at[target], other
+            parts.at[slot, 1 - mine, group(h)],
+            arrived.at[target, group(h)],
+            part_send.at[slot, h],
+            part_recv.at[target, h],
+            other,
         )
 
-    def left(c):
-        slot = lax.rem(c, 2)
-
-        @pl.when(c >= 2)
-        def _():
-            part_copy(c - 2).wait_send()
-
-        rows_copy(c).wait()
-
-        @pl.when(c + 1 < chunks)
-        def _():
-            rows_copy(c + 1).start()
-
-        def one(p, carry):
-            value = jnp.dot(rows_buf[slot], psi[p], preferred_element_type=jnp.float32)
+    def left_block(c, n, h):
+        slot = lax.rem(c, AHEAD)
+        source = lax.rem(n, 2)
+
+        def one(s, carry):
+            p = h * states + s
+            value = jnp.dot(rows_buf[source], psi[p], preferred_element_type=jnp.float32)
             value = value.astype(jnp.bfloat16)
             rows = value.shape[0] // 2
             parts[slot, 0, p] = value[:rows]
             parts[slot, 1, p] = value[rows:]
             return carry
 
-        lax.fori_loop(0, pairs, one, 0)
-        part_copy(c).start()
-
-    def front(c):
+        lax.fori_loop(0, states, one, 0)
+        part_copy(c, h).start()
+
+    share.wait()
+    for h in range(blocks):
+        psi_copies[h].wait()
+        if h == blocks - 1:
+            for copy in across_copies:
+                copy.start()
+        relay = remote(
+            psi.at[group(h), across_span, :], psi.at[group(h), across_span, :], relay_send.at[h], relay_recv.at[h], partner
+        )
+        relay.start()
+        if h == 0:
+            for copy in beside_copies:
+                copy.start()
+        relay.wait()
+
+        def one(c, carry):
+            n = h * AHEAD + c
+            rows_copy(n, c).wait()
+            rows_copy(n + 1, jnp.where(n == blocks * AHEAD - 1, AHEAD, lax.rem(c + 1, AHEAD))).start()
+            left_block(c, n, h)
+            return carry
+
+        lax.fori_loop(0, AHEAD, one, 0)
+
+    def left(c):
+        n = c + (blocks - 1) * AHEAD
+        for h in range(blocks):
+            part_copy(c - AHEAD, h).wait_send()
+
+        @pl.when(c > AHEAD)
+        def _():
+            pl.semaphore_wait(part_free, 1)
+
+        rows_copy(n, c).wait()
+
         @pl.when(c + 1 < chunks)
         def _():
-            left(c + 1)
-
-        part_copy(c).wait_recv()
-        slot = lax.rem(c, 2)
-        source = lax.rem(c, 4)
-        target = lax.rem(c, DEPTH)
+            rows_copy(n + 1, c + 1).start()
+
+        for h in range(blocks):
+            left_block(c, n, h)
+
+    def front(c):
+        slot = lax.rem(c, AHEAD)
+        source = lax.rem(c, AHEAD + 1)
+        target = lax.rem(c, kept)
         tile = 16
         wide = psi.shape[2]
 
         def one(h, carry):
+            part_copy(c, h).wait_recv()
             for step in range(STEP // tile):
                 planes = []
                 for w in range(width):
@@ -324,9 +453,13 @@
 
         lax.fori_loop(0, blocks, one, 0)
 
+        @pl.when(c + AHEAD + 1 < chunks)
+        def _():
+            pl.semaphore_signal(part_free, inc=1, device_id=other, device_id_type=MESH)
+
     def up_copy(u, d):
         slot = lax.rem(u, DEPTH)
-        return remote(sums.at[slot, d], from_low.at[slot, d], sum_send.at[slot, d], low_recv.at[slot, d], higher)
+        return remote(sums.at[slot, d], from_low.at[slot, d - 1], sum_send.at[slot, d], low_recv.at[slot, d - 1], higher)
 
     def down_copy(u, d):
         slot = lax.rem(u, DEPTH)
@@ -343,45 +476,40 @@
             def _():
                 down_copy(u, d).wait_send()
 
-    def added(slot, d, source):
-        total = sums[slot, d].astype(jnp.float32) + source[slot, d].astype(jnp.float32)
+    def added(slot, d, source, n):
+        total = sums[slot, d].astype(jnp.float32) + source[slot, n].astype(jnp.float32)
         sums[slot, d] = total.astype(jnp.bfloat16)
 
     def where_to(u):
-        near = jnp.where(u < 2 * early, 1, 0)
-        first = jnp.where(u < 3 * early, 1, 0)
-        second = jnp.where(u < 6 * early, 1, 0)
-        third = jnp.where(u < 8 * early, 1, 0)
-        a, b, e, g = u, u - 2 * early, u - 3 * early, u - 6 * early
-        f = u - 8 * early
-        chunk = jnp.where(
-            near == 1,
-            a // 2,
-            jnp.where(
-                first == 1,
-                b,
-                jnp.where(second == 1, early + e // 3, jnp.where(third == 1, g, 2 * early + f // 4)),
-            ),
-        )
-        kind = jnp.where(
-            near == 1,
-            lax.rem(a, 2),
-            jnp.where(
-                first == 1, 2, jnp.where(second == 1, lax.rem(e + 3 * units, 3), jnp.where(third == 1, 3, lax.rem(f + 8 * units, 4)))
-            ),
-        )
+        second, third, fourth = 3 * early, 3 * early + 3 * middle, 4 * (early + middle)
+        e, f = lax.rem(u + 3 * units - second, 3), lax.rem(u + 4 * units - fourth, 4)
+        chunk = jnp.where(u < fourth, u - third, kept + (u - fourth) // 4)
+        chunk = jnp.where(u < third, early + (u - second) // 3, chunk)
+        chunk = jnp.where(u < second, u - 2 * early, chunk)
+        chunk = jnp.where(u < 2 * early, u // 2, chunk)
+        kind = jnp.where(u < fourth, 3, f)
+        kind = jnp.where(u < third, e, kind)
+        kind = jnp.where(u < second, 2, kind)
+        kind = jnp.where(u < 2 * early, lax.rem(u, 2), kind)
         return chunk, kind
 
-    def done_copies(u):
-        slot = lax.rem(u, 2)
+    def places(u):
         chunk, kind = where_to(u)
         far = kind // 2
         near_block = here + kind * (beside - here)
-        copies = []
+        spots = []
         for j in range(2):
             far_block = corner if j else across
             block = (1 - far) * near_block + far * far_block
             column = (1 - far) * j + far * (kind - 2)
+            spots.append((block, column))
+        return chunk, spots
+
+    def done_copies(u):
+        slot = lax.rem(u, 2)
+        chunk, spots = places(u)
+        copies = []
+        for j, (block, column) in enumerate(spots):
             copies.append(
                 pltpu.make_async_copy(
                     done.at[slot, j],
@@ -396,6 +524,18 @@
             )
         return copies
 
+    def gather_terms(u):
+        slot = lax.rem(u, 2)
+        chunk, spots = places(u)
+        first = pl.multiple_of(here * depth + chunk * STEP, STEP)
+        for j, (block, column) in enumerate(spots):
+            for t in range(states):
+                value = done[slot, j, t]
+                start = psi[block * states + t, pl.ds(first, STEP), pl.ds(pl.multiple_of(column * half, half), half)]
+                start = start.astype(jnp.float32)
+                terms[1] += folded(start * value)
+                terms[2] += folded(value * value)
+
     def handle(i):
         up = i - HOP * place
         slot_up = lax.rem(up + DEPTH * HOP * line, DEPTH)
@@ -413,7 +553,7 @@
                     @pl.when(place > 0)
                     def _():
                         up_copy(up, d).wait_recv()
-                        added(slot_up, d, from_low)
+                        added(slot_up, d, from_low, d - 1)
 
                     up_copy(up, d).start()
 
@@ -433,7 +573,7 @@
                     @pl.when(place < line - 1)
                     def _():
                         down_copy(down, d).wait_recv()
-                        added(slot_down, d, from_high)
+                        added(slot_down, d, from_high, d)
 
                     down_copy(down, d).start()
 
@@ -456,7 +596,7 @@
             @pl.when(place > 0)
             def _():
                 up_copy(last, place).wait_recv()
-                more = from_low[slot, place].astype(jnp.float32)
+                more = from_low[slot, place - 1].astype(jnp.float32)
                 done[spot] = done[spot] + more.reshape(shape)
 
                 @pl.when(last < units - DEPTH)
@@ -475,6 +615,7 @@
 
             for copy in done_copies(last):
                 copy.start()
+            gather_terms(last)
 
     def unit(u, c, kind):
         slot = lax.rem(u, DEPTH)
@@ -483,7 +624,7 @@
         def _():
             drained(u - DEPTH)
 
-        source = lax.rem(c, DEPTH)
+        source = lax.rem(c, kept)
 
         def one(j, carry):
             value = jnp.dot(mixed[source], images[2 * kind + j], preferred_element_type=jnp.float32)
@@ -506,11 +647,16 @@
                 return carry
 
             lax.fori_loop(0, len(kinds), inner, 0)
+            if fresh:
+
+                @pl.when(c + AHEAD < chunks)
+                def _():
+                    left(c + AHEAD)
+
             return carry
 
         return one
 
-    left(0)
     for copy in beside_copies:
         copy.wait()
     lax.fori_loop(0, early, walk(0, 0, (0, 1), True), 0)
@@ -518,33 +664,56 @@
     corner_copies[0].start()
     corner_copies[0].wait()
     lax.fori_loop(0, early, walk(0, 2 * early, (2,), False), 0)
-    lax.fori_loop(0, early, walk(early, 3 * early, (0, 1, 2), True), 0)
+    lax.fori_loop(0, middle, walk(early, 3 * early, (0, 1, 2), True), 0)
     across_copies[1].wait()
     corner_copies[1].start()
     corner_copies[1].wait()
-    lax.fori_loop(0, 2 * early, walk(0, 6 * early, (3,), False), 0)
-    lax.fori_loop(0, 2 * early, walk(2 * early, 8 * early, (0, 1, 2, 3), True), 0)
+    lax.fori_loop(0, kept, walk(0, 3 * kept, (3,), False), 0)
+    lax.fori_loop(0, chunks - kept, walk(kept, 4 * kept, (0, 1, 2, 3), True), 0)
 
     def finish(i, carry):
         handle(i)
         return carry
 
     lax.fori_loop(units, units + HOP * (line - 1), finish, 0)
+    for n, device in enumerate((partner, opposite, other, paired, distant)):
+        copy = remote(terms, heard.at[n], term_send.at[n], term_recv.at[n], device)
+        copy.start()
+        copy.wait()
+        terms[...] = terms[...] + heard[n]
+
+    def whole(n):
+        value = jnp.sum(terms[n], axis=1, keepdims=True)
+        return jnp.sum(value, axis=0, keepdims=True) / entries
+
+    norm_sq = whole(0) + EPSILON
+    projection = whole(1)
+    alpha_coef = projection / norm_sq
+    beta_coef = jnp.sqrt((whole(2) - alpha_coef * projection) / norm_sq + EPSILON)
+    scale = 1.0 / (jnp.sqrt(norm_sq) * beta_coef)
+    for n, value in enumerate((alpha_coef, beta_coef, scale)):
+        total_ref[n] = jnp.broadcast_to(value, total_ref.shape[1:])
     for u in range(units - DEPTH, units):
         drained(u)
     for u in range(units - 2, units):
         for copy in done_copies(u):
             copy.wait()
-    for c in range(chunks - 2, chunks):
-        part_copy(c).wait_send()
-
-
-def line_call(pair, own, near, far, env, right, line):
+    for c in range(chunks - AHEAD, chunks):
+        for h in range(blocks):
+            part_copy(c, h).wait_send()
+
+
+def early_chunks(chunks):
+    return 6 * chunks // 16, 3 * chunks // 16
+
+
+def line_call(pair, own, left, right, line, lefts, blocks, entries):
     pairs, depth, wide = own.shape
-    chunks, rows, inner = env.shape
-    width = rows // (2 * STEP)
-    blocks = inner // depth
     states = pairs // blocks
+    inner = blocks * depth
+    width = left.shape[0] // inner
+    chunks = left.shape[1] // (lefts * STEP)
+    rows = lefts * width * STEP
     lanes = right.shape[1] // line
     half = lanes // 2
     tall = states * STEP
@@ -553,46 +722,60 @@
     dma = pltpu.SemaphoreType.DMA
     plain = pltpu.SemaphoreType.REGULAR
     return pl.pallas_call(
-        functools.partial(line_kernel, (width, blocks, states, depth, line)),
-        out_shape=jax.ShapeDtypeStruct((blocks, states, chunks * STEP, lanes), jnp.float32),
-        in_specs=[pl.BlockSpec(memory_space=pltpu.SMEM)] + [hbm] * 5,
-        out_specs=hbm,
+        functools.partial(line_kernel, (width, blocks, states, depth, line, entries)),
+        out_shape=(
+            jax.ShapeDtypeStruct((blocks, states, chunks * STEP, lanes), jnp.float32),
+            jax.ShapeDtypeStruct((chunks, rows, inner), low),
+            jax.ShapeDtypeStruct((3, 8, LANES), jnp.float32),
+        ),
+        in_specs=[pl.BlockSpec(memory_space=pltpu.SMEM)] + [hbm] * 3,
+        out_specs=(hbm, hbm, pl.BlockSpec(memory_space=pltpu.VMEM)),
         scratch_shapes=[
             pltpu.VMEM((pairs, inner, wide), low),
             pltpu.VMEM((8, right.shape[0], line * half), low),
-            pltpu.VMEM((DEPTH, tall, right.shape[0]), low),
+            pltpu.VMEM((sum(early_chunks(chunks)), tall, right.shape[0]), low),
+            pltpu.VMEM((2, inner, LANES), low),
             pltpu.VMEM((2, rows, inner), low),
-            pltpu.VMEM((2, 2, pairs, rows // 2, wide), low),
-            pltpu.VMEM((4, pairs, rows // 2, wide), low),
+            pltpu.VMEM((AHEAD, 2, pairs, rows // 2, wide), low),
+            pltpu.VMEM((AHEAD + 1, pairs, rows // 2, wide), low),
             pltpu.VMEM((DEPTH, line, 2, tall, half), low),
-            pltpu.VMEM((DEPTH, line, 2, tall, half), low),
-            pltpu.VMEM((DEPTH, line, 2, tall, half), low),
+            pltpu.VMEM((DEPTH, line - 1, 2, tall, half), low),
+            pltpu.VMEM((DEPTH, line - 1, 2, tall, half), low),
             pltpu.VMEM((2, 2, states, STEP, half), jnp.float32),
-            dma((3,)),
+            pltpu.VMEM((3, 8, LANES), jnp.float32),
+            pltpu.VMEM((5, 3, 8, LANES), jnp.float32),
             dma((1,)),
-            dma((1,)),
+            dma((blocks + 1,)),
+            dma((blocks + 1,)),
+            dma((blocks,)),
+            dma((blocks,)),
             dma((2, line)),
             dma((6,)),
             dma((6,)),
             dma((2,)),
+            dma((2, LANES // STEP)),
             dma((2,)),
-            dma((4,)),
+            dma((AHEAD, blocks)),
+            dma((AHEAD + 1, blocks)),
+            plain,
             dma((DEPTH, line)),
-            dma((DEPTH, line)),
-            dma((DEPTH, line)),
+            dma((DEPTH, line - 1)),
+            dma((DEPTH, line - 1)),
             plain,
             plain,
             dma((2, 2)),
+            dma((5,)),
+            dma((5,)),
         ],
         compiler_params=pltpu.CompilerParams(
             collective_id=0, has_side_effects=True, vmem_limit_bytes=67043328
         ),
         cost_estimate=pl.CostEstimate(
             flops=2 * chunks * (rows * inner * pairs * wide + tall * right.shape[0] * 4 * line * lanes),
-            bytes_accessed=2 * (env.size + 3 * own.size + right.size) + 4 * chunks * tall * blocks * lanes,
+            bytes_accessed=4 * (left.size + own.size + right.size) + 4 * chunks * tall * blocks * lanes,
             transcendentals=0,
         ),
-    )(pair.reshape(-1), own, near, far, env, right)
+    )(pair.reshape(-1), own, left, right)
 
 
 def lined_body(state, left_env, right_env, site_one, site_two):
@@ -600,35 +783,12 @@
     lefts, rights, owners = (lax.axis_size(name) for name in ("lb", "rb", "wa"))
     _, blocks, states, depth, lanes = state.shape
     entries = float(state.size * lefts * rights * owners)
-    width, _, _, _, rows = left_env.shape
     own = state.reshape(blocks * states, depth, lanes)
-    far = lax.ppermute(own, "wa", [(a, (a + 2) % 4) for a in range(owners)])
-    near = lax.ppermute(own, "wa", [(a, a ^ 1) for a in range(owners)])
-    chunks = rows // (lefts * STEP)
-    env = left_env.reshape(width, blocks, depth, lefts, chunks, STEP)
-    env = jnp.transpose(env, (4, 3, 0, 5, 1, 2)).reshape(chunks, lefts * width * STEP, blocks * depth)
+    left = left_env.reshape(-1, left_env.shape[-1])
     right = right_env.reshape(-1, right_env.shape[-1])
-    applied = line_call(pair, own, near, far, env, right, rights)
-    state_values = state[0].astype(jnp.float32)
-    terms = jnp.stack(
-        [
-            jnp.sum(state_values * state_values),
-            jnp.sum(state_values * applied),
-            jnp.sum(applied * applied),
-        ]
-    )
-    for name in ("wa", "lb", "rb"):
-        size, bit = lax.axis_size(name), 1
-        while bit < size:
-            terms = terms + lax.ppermute(terms, name, [(a, a ^ bit) for a in range(size)])
-            bit *= 2
-    squares, crossed, image_squares = terms
-    norm_sq = squares / entries + EPSILON
-    projection = crossed / entries
-    alpha_coef = projection / norm_sq
-    beta_coef = jnp.sqrt((image_squares / entries - alpha_coef * projection) / norm_sq + EPSILON)
-    scale = 1.0 / (jnp.sqrt(norm_sq) * beta_coef)
-    result = (applied - alpha_coef * state_values) * scale
+    applied, _, totals = line_call(pair, own, left, right, rights, lefts, blocks, entries)
+    alpha_coef, beta_coef, scale = totals[0, 0, 0], totals[1, 0, 0], totals[2, 0, 0]
+    result = (applied - alpha_coef * state[0].astype(jnp.float32)) * scale
     return (result[None], jnp.stack([alpha_coef, beta_coef]))
 
 

time: 496 us -> 447 us (0.901)
  Pallas kernels: 358 us -> 430 us
  local copies, waits for them, and re-layouts: 55.1 us -> 2.28 us
  waiting for transfers between devices: 49.2 us -> 0 us
  other arithmetic: 22.3 us -> 12.4 us
  starting transfers between devices: 6.86 us -> 0 us
    pallas_call x1, Pallas kernels: 358 us -> 430 us  [line_call(): pl.pallas_call(functools.partial(line_kernel, (width, blocks, states, dep...]
    ppermute x7 -> x0, waiting for transfers between devices: 49.2 us -> none  [the longest x1 36.6 us: lined_body(): far = lax.ppermute(own, 'wa', [(a, (a + 2) % 4) for a in range(owners)])]
    reshape x1 -> x0, local copies, waits for them, and re-layouts: 20.9 us -> none  [lined_body(): jnp.transpose(env, (4, 3, 0, 5, 1, 2))]
    unnamed x5 -> x0, local copies, waits for them, and re-layouts: 16.9 us -> none
    transpose x1 -> x0, local copies, waits for them, and re-layouts: 15.6 us -> none  [lined_body(): jnp.transpose(env, (4, 3, 0, 5, 1, 2))]
    ppermute x7 -> x0, starting transfers between devices: 6.86 us -> none  [the longest x5 3.74 us: lined_body(): lax.ppermute(terms, name, [(a, a ^ bit) for a in range(size)])]
    reduce_sum x1 -> x0, other arithmetic: 6.43 us -> none  [lined_body(): jnp.sum(state_values * applied)]
  transfers between devices with their start and end apart: 7 -> 0, of which waited for: 6 -> 0; matrix products, arithmetic and copies ran while one was open for 11% -> 0% of each run, Pallas kernels for 0% -> 0%
where the time goes in v1:
time: 447 us; the launch traced here: 446 us
  Pallas kernels  430 us (96%)
  other arithmetic  12.4 us (3%)
    pallas_call x1, Pallas kernels, line_call(): pl.pallas_call(functools.partial(line_kernel, (width, blocks, states, dep...  430 us
    broadcast_in_dim x1, other arithmetic, lined_body(): return (result[None], jnp.stack([alpha_coef, beta_coef]))  10.5 us

profile of v1, /device:TPU:0, one launch (start us, length us, event | category | flops | bytes accessed | tf_op | source)
XLA Modules:
  0.0 446.1 jit_solution(8774963878545279111)
XLA Ops:
  0.6 1.1 convolution_bitcast_fusion
  1.8 0.3 copy.11
  2.0 0.7 reshape_reshape.3.pair_ref
  2.7 429.7 %shard_map.68 = (f32[4,4,512,256]{3,2,1,0:T(8,128)}, bf16[16,192,2048]{2,1,0:T(8,128)(2,1)}, f32[3,8,128]{2,1,0:T(8,128)}) custom-call(f32[144]{0:T(256)} %reshape_reshape.3.pair_ref, bf16[16,512,256]{2,1,0:T(8,128)(2,1)} %bitcast.19, bf16[6144,1024]{1,0:T(8,128)(2,1)} %bitcast.22, bf16[3072,1024]{1,0:T(8,128)(2,1)} %bitcast.23), custom_call_target="tpu_custom_call" | custom-call | flops 103079215104 | bytes 54525952 | tf_op jit(solution)/shard_map/pallas_call | solution.py:724
  432.4 1.3 fusion.4
  433.7 1.9 pad_maximum_fusion
  435.6 10.5 %fusion.1 = f32[1,4,4,512,256]{4,3,2,1,0:T(8,128)} fusion(f32[4,4,512,256]{3,2,1,0:T(8,128)} %get-tuple-element.4, bf16[1,4,4,512,256]{4,3,2,1,0:T(8,128)(2,1)} %param.5, f32[]{:T(128)} %bitcast.8, f32[]{:T(128)} %bitcast.6), kind=kLoop, calls=%fused_computation.2 | loop fusion | flops 8388608 | bytes 20971528 | tf_op jit(solution)/shard_map/broadcast_in_dim | solution.py:792

commit v2 on v1

--- a/solution.py
+++ b/solution.py
@@ -152,7 +152,8 @@
 STEP = 32
 DEPTH = 8
 HOP = 2
-AHEAD = 3
+AHEAD = 4
+CUT = 2
 LANES = 128
 
 
@@ -176,6 +177,7 @@
     from_low,
     from_high,
     done,
+    ready,
     terms,
     heard,
     load_sem,
@@ -207,6 +209,7 @@
     early, middle = early_chunks(chunks)
     kept = early + middle
     inner = blocks * depth
+    piece = inner // CUT
     mine = lax.axis_index("lb")
     place = lax.axis_index("rb")
     here = lax.axis_index("wa")
@@ -218,8 +221,8 @@
     other = (1 - mine, place, here)
     higher = (mine, lax.rem(place + 1, line), here)
     lower = (mine, lax.rem(place + line - 1, line), here)
-    paired = (mine, place + 1 - 2 * lax.rem(place, 2), here)
-    distant = (mine, lax.rem(place + 2, line), here)
+    turned_line = [(mine, lax.rem(place + k, line), here) for k in range(1, line)]
+    turned_blocks = [(mine, place, lax.rem(here + k, 4)) for k in range(1, 4)]
 
     def remote(source, target, send, recv, device):
         return pltpu.make_async_remote_copy(
@@ -233,12 +236,12 @@
 
     def raw_copy(n):
         slot = lax.rem(n, 2)
-        q = n // (2 * width)
-        side = lax.rem(n // width, 2)
-        w = lax.rem(n, width)
+        q = n // (2 * width * CUT)
+        side = lax.rem(n // (width * CUT), 2)
+        row = lax.rem(n, width * CUT) * piece
         first = side * (chunks * STEP) + q * LANES
         return pltpu.make_async_copy(
-            left_ref.at[pl.ds(pl.multiple_of(w * inner, inner), inner), pl.ds(pl.multiple_of(first, LANES), LANES)],
+            left_ref.at[pl.ds(pl.multiple_of(row, piece), piece), pl.ds(pl.multiple_of(first, LANES), LANES)],
             raw.at[slot],
             raw_sem.at[slot],
         )
@@ -246,7 +249,7 @@
     raw_copy(0).start()
 
     barrier = pltpu.get_barrier_semaphore()
-    devices = (partner, opposite, other, higher, lower, distant)
+    devices = turned_line + turned_blocks + [other]
     for device in devices:
         pl.semaphore_signal(barrier, inc=1, device_id=device, device_id_type=MESH)
     pl.semaphore_wait(barrier, len(devices))
@@ -278,19 +281,20 @@
     for copy in local:
         copy.start()
 
-    turns = 2 * width * chunks * STEP // LANES
+    turns = 2 * width * CUT * chunks * STEP // LANES
     cuts = LANES // STEP
 
     def turned_copies(n):
         slot = lax.rem(n, 2)
-        q = n // (2 * width)
-        side = lax.rem(n // width, 2)
-        w = lax.rem(n, width)
+        q = n // (2 * width * CUT)
+        side = lax.rem(n // (width * CUT), 2)
+        w = lax.rem(n // CUT, width)
         first = (side * width + w) * STEP
+        column = pl.multiple_of(lax.rem(n, CUT) * piece, piece)
         return [
             pltpu.make_async_copy(
-                mixed.at[slot, pl.ds(k * STEP, STEP), pl.ds(0, inner)],
-                env_ref.at[q * cuts + k, pl.ds(pl.multiple_of(first, STEP), STEP), :],
+                mixed.at[slot, pl.ds(k * STEP, STEP), pl.ds(0, piece)],
+                env_ref.at[q * cuts + k, pl.ds(pl.multiple_of(first, STEP), STEP), pl.ds(column, piece)],
                 turn_sem.at[slot, k],
             )
             for k in range(cuts)
@@ -310,7 +314,7 @@
             for copy in turned_copies(n - 2):
                 copy.wait()
 
-        for g in range(blocks):
+        for g in range(blocks // CUT):
             span = pl.ds(g * depth, depth)
             mixed[slot, pl.ds(0, LANES), span] = raw[slot, span, :].T
         for copy in turned_copies(n):
@@ -353,7 +357,7 @@
 
     def part_copy(c, h):
         slot = lax.rem(c, AHEAD)
-        target = lax.rem(c, AHEAD + 1)
+        target = lax.rem(c, AHEAD)
         return remote(
             parts.at[slot, 1 - mine, group(h)],
             arrived.at[target, group(h)],
@@ -407,10 +411,7 @@
         for h in range(blocks):
             part_copy(c - AHEAD, h).wait_send()
 
-        @pl.when(c > AHEAD)
-        def _():
-            pl.semaphore_wait(part_free, 1)
-
+        pl.semaphore_wait(part_free, 1)
         rows_copy(n, c).wait()
 
         @pl.when(c + 1 < chunks)
@@ -422,7 +423,7 @@
 
     def front(c):
         slot = lax.rem(c, AHEAD)
-        source = lax.rem(c, AHEAD + 1)
+        source = lax.rem(c, AHEAD)
         target = lax.rem(c, kept)
         tile = 16
         wide = psi.shape[2]
@@ -453,7 +454,7 @@
 
         lax.fori_loop(0, blocks, one, 0)
 
-        @pl.when(c + AHEAD + 1 < chunks)
+        @pl.when(c + AHEAD < chunks)
         def _():
             pl.semaphore_signal(part_free, inc=1, device_id=other, device_id_type=MESH)
 
@@ -512,7 +513,7 @@
         for j, (block, column) in enumerate(spots):
             copies.append(
                 pltpu.make_async_copy(
-                    done.at[slot, j],
+                    ready.at[slot, j],
                     out_ref.at[
                         block,
                         :,
@@ -530,7 +531,8 @@
         first = pl.multiple_of(here * depth + chunk * STEP, STEP)
         for j, (block, column) in enumerate(spots):
             for t in range(states):
-                value = done[slot, j, t]
+                value = done[j, t]
+                ready[slot, j, t] = value.astype(ready.dtype)
                 start = psi[block * states + t, pl.ds(first, STEP), pl.ds(pl.multiple_of(column * half, half), half)]
                 start = start.astype(jnp.float32)
                 terms[1] += folded(start * value)
@@ -582,22 +584,21 @@
         @pl.when(last >= 0)
         def _():
             slot = lax.rem(last, DEPTH)
-            spot = lax.rem(last, 2)
 
             @pl.when(last >= 2)
             def _():
                 for copy in done_copies(last - 2):
                     copy.wait()
 
-            shape = done.shape[1:]
+            shape = done.shape
             value = sums[slot, place].astype(jnp.float32)
-            done[spot] = value.reshape(shape)
+            done[...] = value.reshape(shape)
 
             @pl.when(place > 0)
             def _():
                 up_copy(last, place).wait_recv()
                 more = from_low[slot, place - 1].astype(jnp.float32)
-                done[spot] = done[spot] + more.reshape(shape)
+                done[...] = done[...] + more.reshape(shape)
 
                 @pl.when(last < units - DEPTH)
                 def _():
@@ -607,15 +608,15 @@
             def _():
                 down_copy(last, place).wait_recv()
                 more = from_high[slot, place].astype(jnp.float32)
-                done[spot] = done[spot] + more.reshape(shape)
+                done[...] = done[...] + more.reshape(shape)
 
                 @pl.when(last < units - DEPTH)
                 def _():
                     pl.semaphore_signal(low_free, inc=1, device_id=higher, device_id_type=MESH)
 
+            gather_terms(last)
             for copy in done_copies(last):
                 copy.start()
-            gather_terms(last)
 
     def unit(u, c, kind):
         slot = lax.rem(u, DEPTH)
@@ -676,20 +677,33 @@
         return carry
 
     lax.fori_loop(units, units + HOP * (line - 1), finish, 0)
-    for n, device in enumerate((partner, opposite, other, paired, distant)):
-        copy = remote(terms, heard.at[n], term_send.at[n], term_recv.at[n], device)
-        copy.start()
-        copy.wait()
-        terms[...] = terms[...] + heard[n]
+    first = 0
+    for index, peers in ((place, turned_line), (here, turned_blocks), (mine, [other])):
+        heard[first + index] = terms[...]
+        copies = [
+            remote(terms, heard.at[first + index], term_send.at[first + k], term_recv.at[first + k], device)
+            for k, device in enumerate(peers)
+        ]
+        for copy in copies:
+            copy.start()
+        for copy in copies:
+            copy.wait()
+        value = heard[first]
+        for k in range(len(peers)):
+            value = value + heard[first + 1 + k]
+        terms[...] = value
+        first += len(peers) + 1
 
     def whole(n):
         value = jnp.sum(terms[n], axis=1, keepdims=True)
         return jnp.sum(value, axis=0, keepdims=True) / entries
 
-    norm_sq = whole(0) + EPSILON
+    mean_sq = whole(0)
+    norm_sq = mean_sq + EPSILON
     projection = whole(1)
     alpha_coef = projection / norm_sq
-    beta_coef = jnp.sqrt((whole(2) - alpha_coef * projection) / norm_sq + EPSILON)
+    left_over = whole(2) - 2.0 * alpha_coef * projection + alpha_coef * alpha_coef * mean_sq
+    beta_coef = jnp.sqrt(jnp.maximum(left_over, 0.0) / norm_sq + EPSILON)
     scale = 1.0 / (jnp.sqrt(norm_sq) * beta_coef)
     for n, value in enumerate((alpha_coef, beta_coef, scale)):
         total_ref[n] = jnp.broadcast_to(value, total_ref.shape[1:])
@@ -724,7 +738,7 @@
     return pl.pallas_call(
         functools.partial(line_kernel, (width, blocks, states, depth, line, entries)),
         out_shape=(
-            jax.ShapeDtypeStruct((blocks, states, chunks * STEP, lanes), jnp.float32),
+            jax.ShapeDtypeStruct((blocks, states, chunks * STEP, lanes), low),
             jax.ShapeDtypeStruct((chunks, rows, inner), low),
             jax.ShapeDtypeStruct((3, 8, LANES), jnp.float32),
         ),
@@ -734,16 +748,17 @@
             pltpu.VMEM((pairs, inner, wide), low),
             pltpu.VMEM((8, right.shape[0], line * half), low),
             pltpu.VMEM((sum(early_chunks(chunks)), tall, right.shape[0]), low),
-            pltpu.VMEM((2, inner, LANES), low),
+            pltpu.VMEM((2, inner // CUT, LANES), low),
             pltpu.VMEM((2, rows, inner), low),
             pltpu.VMEM((AHEAD, 2, pairs, rows // 2, wide), low),
-            pltpu.VMEM((AHEAD + 1, pairs, rows // 2, wide), low),
+            pltpu.VMEM((AHEAD, pairs, rows // 2, wide), low),
             pltpu.VMEM((DEPTH, line, 2, tall, half), low),
             pltpu.VMEM((DEPTH, line - 1, 2, tall, half), low),
             pltpu.VMEM((DEPTH, line - 1, 2, tall, half), low),
-            pltpu.VMEM((2, 2, states, STEP, half), jnp.float32),
+            pltpu.VMEM((2, states, STEP, half), jnp.float32),
+            pltpu.VMEM((2, 2, states, STEP, half), low),
             pltpu.VMEM((3, 8, LANES), jnp.float32),
-            pltpu.VMEM((5, 3, 8, LANES), jnp.float32),
+            pltpu.VMEM((line + 6, 3, 8, LANES), jnp.float32),
             dma((1,)),
             dma((blocks + 1,)),
             dma((blocks + 1,)),
@@ -756,7 +771,7 @@
             dma((2, LANES // STEP)),
             dma((2,)),
             dma((AHEAD, blocks)),
-            dma((AHEAD + 1, blocks)),
+            dma((AHEAD, blocks)),
             plain,
             dma((DEPTH, line)),
             dma((DEPTH, line - 1)),
@@ -764,8 +779,8 @@
             plain,
             plain,
             dma((2, 2)),
-            dma((5,)),
-            dma((5,)),
+            dma((line + 6,)),
+            dma((line + 6,)),
         ],
         compiler_params=pltpu.CompilerParams(
             collective_id=0, has_side_effects=True, vmem_limit_bytes=67043328
@@ -787,9 +802,29 @@
     left = left_env.reshape(-1, left_env.shape[-1])
     right = right_env.reshape(-1, right_env.shape[-1])
     applied, _, totals = line_call(pair, own, left, right, rights, lefts, blocks, entries)
-    alpha_coef, beta_coef, scale = totals[0, 0, 0], totals[1, 0, 0], totals[2, 0, 0]
-    result = (applied - alpha_coef * state[0].astype(jnp.float32)) * scale
-    return (result[None], jnp.stack([alpha_coef, beta_coef]))
+    return final_call(totals, applied, state)
+
+
+def final_kernel(total_ref, applied_ref, state_ref, out_ref, coef_ref):
+    alpha_coef, scale = total_ref[0, 0, 0], total_ref[2, 0, 0]
+    state_values = state_ref[0].astype(jnp.float32)
+    out_ref[0] = (applied_ref[...].astype(jnp.float32) - alpha_coef * state_values) * scale
+    for n in range(2):
+        coef_ref[n] = total_ref[n, 0, 0]
+
+
+def final_call(totals, applied, state):
+    _, blocks, states, depth, lanes = state.shape
+    smem = pl.BlockSpec(memory_space=pltpu.SMEM)
+    whole = pl.BlockSpec((1, 1, 1, depth, lanes), lambda h, s: (0, h, s, 0, 0))
+    return pl.pallas_call(
+        final_kernel,
+        grid=(blocks, states),
+        out_shape=(jax.ShapeDtypeStruct(state.shape, jnp.float32), jax.ShapeDtypeStruct((2,), jnp.float32)),
+        in_specs=[smem, pl.BlockSpec((1, 1, depth, lanes), lambda h, s: (h, s, 0, 0)), whole],
+        out_specs=(whole, smem),
+        cost_estimate=pl.CostEstimate(flops=4 * state.size, bytes_accessed=8 * state.size, transcendentals=0),
+    )(totals, applied, state)
 
 
 def fits(mesh):

time: 447 us -> 436 us (0.975)
  other arithmetic: 12.4 us -> 0 us
    pallas_call x0 -> x1, Pallas kernels: none -> 12.3 us  [final_call(): pl.pallas_call(final_kernel, grid=(blocks, states), out_shape=(jax.ShapeD...]
    broadcast_in_dim x1 -> x0, other arithmetic: 10.5 us -> none  [lined_body(): return (result[None], jnp.stack([alpha_coef, beta_coef]))]
    pallas_call x1, Pallas kernels: 430 us -> 420 us  [line_call(): pl.pallas_call(functools.partial(line_kernel, (width, blocks, states, dep...]
where the time goes in v2:
time: 436 us; the launch traced here: 435 us
  Pallas kernels  432 us (99%)
    pallas_call x1, Pallas kernels, line_call(): pl.pallas_call(functools.partial(line_kernel, (width, blocks, states, dep...  420 us
    pallas_call x1, Pallas kernels, final_call(): pl.pallas_call(final_kernel, grid=(blocks, states), out_shape=(jax.ShapeD...  12.3 us

profile of v2, /device:TPU:0, one launch (start us, length us, event | category | flops | bytes accessed | tf_op | source)
XLA Modules:
  0.0 435.1 jit_solution(4766855990466200409)
XLA Ops:
  0.6 1.1 convolution_bitcast_fusion
  1.8 0.3 copy.11
  2.0 0.7 reshape_reshape.3.pair_ref
  2.7 420.1 %shard_map.68 = (bf16[4,4,512,256]{3,2,1,0:T(8,128)(2,1)}, bf16[16,192,2048]{2,1,0:T(8,128)(2,1)}, f32[3,8,128]{2,1,0:T(8,128)}) custom-call(f32[144]{0:T(256)} %reshape_reshape.3.pair_ref, bf16[16,512,256]{2,1,0:T(8,128)(2,1)} %bitcast.7, bf16[6144,1024]{1,0:T(8,128)(2,1)} %bitcast.10, bf16[3072,1024]{1,0:T(8,128)(2,1)} %bitcast.11), custom_call_target="tpu_custom_call" | custom-call | flops 103079215104 | bytes 54525952 | tf_op jit(solution)/shard_map/pallas_call | solution.py:738
  422.8 12.3 %shard_map.69 = (f32[1,4,4,512,256]{4,3,2,1,0:T(8,128)}, f32[2]{0:T(128)}) custom-call(f32[3,8,128]{2,1,0:T(8,128)} %get-tuple-element.4.total_ref, bf16[4,4,512,256]{3,2,1,0:T(8,128)(2,1)} %get-tuple-element.5.applied_ref, bf16[1,4,4,512,256]{4,3,2,1,0:T(8,128)(2,1)} %state_ref.1), custom_call_target="tpu_custom_call" | custom-call | flops 8388608 | bytes 16777216 | tf_op jit(solution)/shard_map/pallas_call | solution.py:820

commit v3 on v2

--- a/solution.py
+++ b/solution.py
@@ -154,6 +154,8 @@
 HOP = 2
 AHEAD = 4
 CUT = 2
+PART = 2
+PIECES = 4
 LANES = 128
 
 
@@ -169,7 +171,6 @@
     psi,
     images,
     mixed,
-    raw,
     rows_buf,
     parts,
     arrived,
@@ -208,6 +209,7 @@
     units = 4 * chunks
     early, middle = early_chunks(chunks)
     kept = early + middle
+    groups = blocks * states // PART
     inner = blocks * depth
     piece = inner // CUT
     mine = lax.axis_index("lb")
@@ -234,19 +236,27 @@
     own_copy = pltpu.make_async_copy(own_ref, psi.at[:, my_span, :], load_sem.at[0])
     own_copy.start()
 
-    def raw_copy(n):
+    tiles = piece // LANES
+
+    def raw_copies(n):
         slot = lax.rem(n, 2)
         q = n // (2 * width * CUT)
         side = lax.rem(n // (width * CUT), 2)
         row = lax.rem(n, width * CUT) * piece
         first = side * (chunks * STEP) + q * LANES
-        return pltpu.make_async_copy(
-            left_ref.at[pl.ds(pl.multiple_of(row, piece), piece), pl.ds(pl.multiple_of(first, LANES), LANES)],
-            raw.at[slot],
-            raw_sem.at[slot],
-        )
-
-    raw_copy(0).start()
+        return [
+            pltpu.make_async_copy(
+                left_ref.at[
+                    pl.ds(pl.multiple_of(row + k * LANES, LANES), LANES), pl.ds(pl.multiple_of(first, LANES), LANES)
+                ],
+                mixed.at[2 + slot, :, pl.ds(k * LANES, LANES)],
+                raw_sem.at[slot, k],
+            )
+            for k in range(tiles)
+        ]
+
+    for copy in raw_copies(0):
+        copy.start()
 
     barrier = pltpu.get_barrier_semaphore()
     devices = turned_line + turned_blocks + [other]
@@ -254,16 +264,16 @@
         pl.semaphore_signal(barrier, inc=1, device_id=device, device_id_type=MESH)
     pl.semaphore_wait(barrier, len(devices))
 
-    def group(h):
-        return pl.ds(h * states, states)
+    def group(g):
+        return pl.ds(g * PART, PART)
 
     psi_copies = [
-        remote(own_ref.at[group(h)], psi.at[group(h), my_span, :], psi_send.at[h], psi_recv.at[h], opposite)
-        for h in range(blocks)
+        remote(own_ref.at[group(g)], psi.at[group(g), my_span, :], psi_send.at[g], psi_recv.at[g], opposite)
+        for g in range(groups)
     ]
     for copy in psi_copies:
         copy.start()
-    share = remote(own_ref, psi.at[:, my_span, :], psi_send.at[blocks], psi_recv.at[blocks], partner)
+    share = remote(own_ref, psi.at[:, my_span, :], psi_send.at[groups], psi_recv.at[groups], partner)
     share.start()
 
     lanes = right_ref.shape[1] // line
@@ -305,18 +315,20 @@
 
         @pl.when(n + 1 < turns)
         def _():
-            raw_copy(n + 1).start()
-
-        raw_copy(n).wait()
+            for copy in raw_copies(n + 1):
+                copy.start()
+
+        for copy in raw_copies(n):
+            copy.wait()
 
         @pl.when(n >= 2)
         def _():
             for copy in turned_copies(n - 2):
                 copy.wait()
 
-        for g in range(blocks // CUT):
-            span = pl.ds(g * depth, depth)
-            mixed[slot, pl.ds(0, LANES), span] = raw[slot, span, :].T
+        for k in range(tiles):
+            span = pl.ds(k * LANES, LANES)
+            mixed[slot, :, span] = mixed[2 + slot, :, span].T
         for copy in turned_copies(n):
             copy.start()
         return carry
@@ -351,27 +363,45 @@
     def image_copy(n, source, target, device):
         return remote(images.at[source], images.at[target], right_send.at[n], right_recv.at[n], device)
 
+    tall = images.shape[1] // PIECES
+
+    def piece_copy(n, source, target, k, device):
+        span = pl.ds(k * tall, tall)
+        return remote(
+            images.at[source, span], images.at[target, span], right_send.at[n + k], right_recv.at[n + k], device
+        )
+
     beside_copies = [image_copy(0, 0, 2, partner), image_copy(1, 1, 3, partner)]
-    across_copies = [image_copy(2, 0, 4, opposite), image_copy(3, 1, 6, opposite)]
-    corner_copies = [image_copy(4, 4, 5, partner), image_copy(5, 6, 7, partner)]
-
-    def part_copy(c, h):
+    across_copies, corner_copies = [], []
+    for part in range(2):
+        n = 2 + 2 * part * PIECES
+        target = 4 + 2 * part
+        across_copies.append([piece_copy(n, part, target, k, opposite) for k in range(PIECES)])
+        corner_copies.append([piece_copy(n + PIECES, target, target + 1, k, partner) for k in range(PIECES)])
+
+    def settle(part):
+        for first, second in zip(across_copies[part], corner_copies[part]):
+            first.wait()
+            second.start()
+        for copy in corner_copies[part]:
+            copy.wait()
+
+    def part_copy(c, g):
         slot = lax.rem(c, AHEAD)
-        target = lax.rem(c, AHEAD)
         return remote(
-            parts.at[slot, 1 - mine, group(h)],
-            arrived.at[target, group(h)],
-            part_send.at[slot, h],
-            part_recv.at[target, h],
+            parts.at[slot, 1 - mine, group(g)],
+            arrived.at[slot, group(g)],
+            part_send.at[slot, g],
+            part_recv.at[slot, g],
             other,
         )
 
-    def left_block(c, n, h):
+    def left_block(c, n, g):
         slot = lax.rem(c, AHEAD)
         source = lax.rem(n, 2)
 
         def one(s, carry):
-            p = h * states + s
+            p = g * PART + s
             value = jnp.dot(rows_buf[source], psi[p], preferred_element_type=jnp.float32)
             value = value.astype(jnp.bfloat16)
             rows = value.shape[0] // 2
@@ -379,47 +409,51 @@
             parts[slot, 1, p] = value[rows:]
             return carry
 
-        lax.fori_loop(0, states, one, 0)
-        part_copy(c, h).start()
+        lax.fori_loop(0, PART, one, 0)
+        part_copy(c, g).start()
 
     share.wait()
-    for h in range(blocks):
-        psi_copies[h].wait()
-        if h == blocks - 1:
-            for copy in across_copies:
+    for g in range(groups):
+        psi_copies[g].wait()
+        if g == groups - 1:
+            for copy in across_copies[0] + across_copies[1]:
                 copy.start()
         relay = remote(
-            psi.at[group(h), across_span, :], psi.at[group(h), across_span, :], relay_send.at[h], relay_recv.at[h], partner
+            psi.at[group(g), across_span, :], psi.at[group(g), across_span, :], relay_send.at[g], relay_recv.at[g], partner
         )
         relay.start()
-        if h == 0:
+        if g == 0:
             for copy in beside_copies:
                 copy.start()
         relay.wait()
 
         def one(c, carry):
-            n = h * AHEAD + c
+            n = g * AHEAD + c
             rows_copy(n, c).wait()
-            rows_copy(n + 1, jnp.where(n == blocks * AHEAD - 1, AHEAD, lax.rem(c + 1, AHEAD))).start()
-            left_block(c, n, h)
+            rows_copy(n + 1, jnp.where(n == groups * AHEAD - 1, AHEAD, lax.rem(c + 1, AHEAD))).start()
+            left_block(c, n, g)
             return carry
 
         lax.fori_loop(0, AHEAD, one, 0)
 
     def left(c):
-        n = c + (blocks - 1) * AHEAD
-        for h in range(blocks):
-            part_copy(c - AHEAD, h).wait_send()
+        n = c + (groups - 1) * AHEAD
+        for g in range(groups):
+            part_copy(c - AHEAD, g).wait_send()
 
         pl.semaphore_wait(part_free, 1)
+
         rows_copy(n, c).wait()
 
         @pl.when(c + 1 < chunks)
         def _():
             rows_copy(n + 1, c + 1).start()
 
-        for h in range(blocks):
-            left_block(c, n, h)
+        def one(g, carry):
+            left_block(c, n, g)
+            return carry
+
+        lax.fori_loop(0, groups, one, 0)
 
     def front(c):
         slot = lax.rem(c, AHEAD)
@@ -429,7 +463,8 @@
         wide = psi.shape[2]
 
         def one(h, carry):
-            part_copy(c, h).wait_recv()
+            for k in range(states // PART):
+                part_copy(c, h * (states // PART) + k).wait_recv()
             for step in range(STEP // tile):
                 planes = []
                 for w in range(width):
@@ -507,32 +542,30 @@
         return chunk, spots
 
     def done_copies(u):
-        slot = lax.rem(u, 2)
         chunk, spots = places(u)
         copies = []
         for j, (block, column) in enumerate(spots):
             copies.append(
                 pltpu.make_async_copy(
-                    ready.at[slot, j],
+                    ready.at[j],
                     out_ref.at[
                         block,
                         :,
                         pl.ds(pl.multiple_of(chunk * STEP, STEP), STEP),
                         pl.ds(pl.multiple_of(column * half, half), half),
                     ],
-                    done_sem.at[slot, j],
+                    done_sem.at[j],
                 )
             )
         return copies
 
     def gather_terms(u):
-        slot = lax.rem(u, 2)
         chunk, spots = places(u)
         first = pl.multiple_of(here * depth + chunk * STEP, STEP)
         for j, (block, column) in enumerate(spots):
             for t in range(states):
                 value = done[j, t]
-                ready[slot, j, t] = value.astype(ready.dtype)
+                ready[j, t] = value.astype(ready.dtype)
                 start = psi[block * states + t, pl.ds(first, STEP), pl.ds(pl.multiple_of(column * half, half), half)]
                 start = start.astype(jnp.float32)
                 terms[1] += folded(start * value)
@@ -585,9 +618,9 @@
         def _():
             slot = lax.rem(last, DEPTH)
 
-            @pl.when(last >= 2)
+            @pl.when(last >= 1)
             def _():
-                for copy in done_copies(last - 2):
+                for copy in done_copies(last - 1):
                     copy.wait()
 
             shape = done.shape
@@ -661,14 +694,10 @@
     for copy in beside_copies:
         copy.wait()
     lax.fori_loop(0, early, walk(0, 0, (0, 1), True), 0)
-    across_copies[0].wait()
-    corner_copies[0].start()
-    corner_copies[0].wait()
+    settle(0)
     lax.fori_loop(0, early, walk(0, 2 * early, (2,), False), 0)
     lax.fori_loop(0, middle, walk(early, 3 * early, (0, 1, 2), True), 0)
-    across_copies[1].wait()
-    corner_copies[1].start()
-    corner_copies[1].wait()
+    settle(1)
     lax.fori_loop(0, kept, walk(0, 3 * kept, (3,), False), 0)
     lax.fori_loop(0, chunks - kept, walk(kept, 4 * kept, (0, 1, 2, 3), True), 0)
 
@@ -709,16 +738,15 @@
         total_ref[n] = jnp.broadcast_to(value, total_ref.shape[1:])
     for u in range(units - DEPTH, units):
         drained(u)
-    for u in range(units - 2, units):
-        for copy in done_copies(u):
-            copy.wait()
+    for copy in done_copies(units - 1):
+        copy.wait()
     for c in range(chunks - AHEAD, chunks):
-        for h in range(blocks):
-            part_copy(c, h).wait_send()
+        for g in range(groups):
+            part_copy(c, g).wait_send()
 
 
 def early_chunks(chunks):
-    return 6 * chunks // 16, 3 * chunks // 16
+    return 6 * chunks // 16, 4 * chunks // 16
 
 
 def line_call(pair, own, left, right, line, lefts, blocks, entries):
@@ -728,6 +756,7 @@
     width = left.shape[0] // inner
     chunks = left.shape[1] // (lefts * STEP)
     rows = lefts * width * STEP
+    groups = pairs // PART
     lanes = right.shape[1] // line
     half = lanes // 2
     tall = states * STEP
@@ -748,7 +777,6 @@
             pltpu.VMEM((pairs, inner, wide), low),
             pltpu.VMEM((8, right.shape[0], line * half), low),
             pltpu.VMEM((sum(early_chunks(chunks)), tall, right.shape[0]), low),
-            pltpu.VMEM((2, inner // CUT, LANES), low),
             pltpu.VMEM((2, rows, inner), low),
             pltpu.VMEM((AHEAD, 2, pairs, rows // 2, wide), low),
             pltpu.VMEM((AHEAD, pairs, rows // 2, wide), low),
@@ -756,29 +784,29 @@
             pltpu.VMEM((DEPTH, line - 1, 2, tall, half), low),
             pltpu.VMEM((DEPTH, line - 1, 2, tall, half), low),
             pltpu.VMEM((2, states, STEP, half), jnp.float32),
-            pltpu.VMEM((2, 2, states, STEP, half), low),
+            pltpu.VMEM((2, states, STEP, half), low),
             pltpu.VMEM((3, 8, LANES), jnp.float32),
             pltpu.VMEM((line + 6, 3, 8, LANES), jnp.float32),
             dma((1,)),
-            dma((blocks + 1,)),
-            dma((blocks + 1,)),
-            dma((blocks,)),
-            dma((blocks,)),
+            dma((groups + 1,)),
+            dma((groups + 1,)),
+            dma((groups,)),
+            dma((groups,)),
             dma((2, line)),
-            dma((6,)),
-            dma((6,)),
-            dma((2,)),
+            dma((2 + 4 * PIECES,)),
+            dma((2 + 4 * PIECES,)),
+            dma((2, inner // CUT // LANES)),
             dma((2, LANES // STEP)),
             dma((2,)),
-            dma((AHEAD, blocks)),
-            dma((AHEAD, blocks)),
+            dma((AHEAD, groups)),
+            dma((AHEAD, groups)),
             plain,
             dma((DEPTH, line)),
             dma((DEPTH, line - 1)),
             dma((DEPTH, line - 1)),
             plain,
             plain,
-            dma((2, 2)),
+            dma((2,)),
             dma((line + 6,)),
             dma((line + 6,)),
         ],
@@ -816,12 +844,12 @@
 def final_call(totals, applied, state):
     _, blocks, states, depth, lanes = state.shape
     smem = pl.BlockSpec(memory_space=pltpu.SMEM)
-    whole = pl.BlockSpec((1, 1, 1, depth, lanes), lambda h, s: (0, h, s, 0, 0))
+    whole = pl.BlockSpec((1, 1, states, depth, lanes), lambda h: (0, h, 0, 0, 0))
     return pl.pallas_call(
         final_kernel,
-        grid=(blocks, states),
+        grid=(blocks,),
         out_shape=(jax.ShapeDtypeStruct(state.shape, jnp.float32), jax.ShapeDtypeStruct((2,), jnp.float32)),
-        in_specs=[smem, pl.BlockSpec((1, 1, depth, lanes), lambda h, s: (h, s, 0, 0)), whole],
+        in_specs=[smem, pl.BlockSpec((1, states, depth, lanes), lambda h: (h, 0, 0, 0)), whole],
         out_specs=(whole, smem),
         cost_estimate=pl.CostEstimate(flops=4 * state.size, bytes_accessed=8 * state.size, transcendentals=0),
     )(totals, applied, state)

time: 436 us -> 435 us (level)
  Pallas kernels: 432 us -> 427 us
    pallas_call x1, Pallas kernels: 12.3 us -> 7.4 us  [final_call(): pl.pallas_call(final_kernel, grid=(blocks,), out_shape=(jax.ShapeDtypeStr...]
where the time goes in v3:
time: 435 us; the launch traced here: 430 us
  Pallas kernels  427 us (98%)
    pallas_call x1, Pallas kernels, line_call(): pl.pallas_call(functools.partial(line_kernel, (width, blocks, states, dep...  420 us

profile of v3, /device:TPU:0, one launch (start us, length us, event | category | flops | bytes accessed | tf_op | source)
XLA Modules:
  0.0 430.2 jit_solution(13067194609219787792)
XLA Ops:
  0.6 1.1 convolution_bitcast_fusion
  1.8 0.3 copy.11
  2.0 0.7 reshape_reshape.3.pair_ref
  2.7 420.0 %shard_map.68 = (bf16[4,4,512,256]{3,2,1,0:T(8,128)(2,1)}, bf16[16,192,2048]{2,1,0:T(8,128)(2,1)}, f32[3,8,128]{2,1,0:T(8,128)}) custom-call(f32[144]{0:T(256)} %reshape_reshape.3.pair_ref, bf16[16,512,256]{2,1,0:T(8,128)(2,1)} %bitcast.7, bf16[6144,1024]{1,0:T(8,128)(2,1)} %bitcast.10, bf16[3072,1024]{1,0:T(8,128)(2,1)} %bitcast.11), custom_call_target="tpu_custom_call" | custom-call | flops 103079215104 | bytes 54525952 | tf_op jit(solution)/shard_map/pallas_call | solution.py:767
  422.8 7.4 %shard_map.69 = (f32[1,4,4,512,256]{4,3,2,1,0:T(8,128)}, f32[2]{0:T(128)}) custom-call(f32[3,8,128]{2,1,0:T(8,128)} %get-tuple-element.4.total_ref, bf16[4,4,512,256]{3,2,1,0:T(8,128)(2,1)} %get-tuple-element.5.applied_ref, bf16[1,4,4,512,256]{4,3,2,1,0:T(8,128)(2,1)} %state_ref.1), custom_call_target="tpu_custom_call" | custom-call | flops 8388608 | bytes 16777216 | tf_op jit(solution)/shard_map/pallas_call | solution.py:848
